TPU v7x, 512 devices: a whole 4x8x8 slice. The times are simulated.
512 devices in a mesh: kgrp: 128 (over y, x, z_hi), img: 4 (over z_lo, core).
Axes of the slice: x: 4, y: 8, z: 8 (z_hi: 4, z_lo: 2; z = z_hi * 2 + z_lo), core: 2. Of those that a mesh axis runs over, the one named last changes fastest.
Arguments:
- vectors: float32 [2, 16, 16384], P(None, 'img', 'kgrp'), may hold values from -6 to 6
- conduction: bfloat16 [256, 2, 8, 4, 4096], P('kgrp', None, None, 'img'), may hold values from -6 to 6
- valence: bfloat16 [256, 2, 8, 4, 4096], P('kgrp', None, None, 'img'), may hold values from -6 to 6
- hole_point: int32 [1], replicated, may hold values from 0 to 16383
- kpoint_grid: int32 [3, 256], replicated, may hold values from 0 to 11
- image_cells: int32 [3, 512], replicated, may hold values from -6 to 6
Outputs:
- psi_real: float32 [16, 4, 4096, 512], P(None, 'img', 'kgrp')
- psi_imag: float32 [16, 4, 4096, 512], P(None, 'img', 'kgrp')
All inputs are finite; a program needn't handle non-finite values.
Results may differ from a plain program's by a relative error of at most 0.0043.
Values may be sent and summed in bfloat16 or wider, within the bound.
A program may use at most 64 MiB of HBM per device.

v0:
```python
import jax
import jax.numpy as jnp
import numpy as np
from jax import lax
from jax.sharding import PartitionSpec as P

NV = 8
NC = 8
cosine_levels = np.cos(2.0 * np.pi * np.arange(12) / 12.0)
sine_levels = np.sin(2.0 * np.pi * np.arange(12) / 12.0)


def phase_table(kpoint_grid, image_cells):
    turn_count = kpoint_grid[0][:, None] * image_cells[0][None, :]
    turn_count = turn_count + kpoint_grid[1][:, None] * image_cells[1][None, :]
    turn_count = turn_count + kpoint_grid[2][:, None] * image_cells[2][None, :]
    turn_count = jnp.mod(turn_count, 12)
    cosine = jnp.zeros(turn_count.shape, jnp.float32)
    sine_part = jnp.zeros(turn_count.shape, jnp.float32)
    for level_index in range(12):
        matches = turn_count == level_index
        cosine = jnp.where(matches, jnp.float32(cosine_levels[level_index]), cosine)
        sine_part = jnp.where(matches, jnp.float32(sine_levels[level_index]), sine_part)
    upper_half = jnp.stack([cosine, sine_part], 1)
    lower_half = jnp.stack([-sine_part, cosine], 1)
    return jnp.stack([upper_half, lower_half], 0).astype(jnp.bfloat16)


def hole_weights(amplitudes, hole_values):
    norm_factor = (NV * NC) ** (-0.5)
    real_amplitude = amplitudes[0]
    imaginary_amplitude = amplitudes[1]
    real_hole = hole_values[:, 0]
    imaginary_hole = hole_values[:, 1]
    highest = lax.Precision.HIGHEST
    weight_real = jnp.einsum("skvc,kv->ksc", real_amplitude, real_hole, precision=highest)
    weight_real = weight_real + jnp.einsum(
        "skvc,kv->ksc", imaginary_amplitude, imaginary_hole, precision=highest
    )
    weight_imaginary = jnp.einsum("skvc,kv->ksc", imaginary_amplitude, real_hole, precision=highest)
    weight_imaginary = weight_imaginary - jnp.einsum(
        "skvc,kv->ksc", real_amplitude, imaginary_hole, precision=highest
    )
    return jnp.stack([weight_real * norm_factor, weight_imaginary * norm_factor], 1).astype(
        jnp.bfloat16
    )


def mixing(weights):
    weight_real = weights[:, 0]
    weight_imaginary = weights[:, 1]
    first_row = jnp.stack([weight_real, -weight_imaginary], 2)
    second_row = jnp.stack([weight_imaginary, weight_real], 2)
    return jnp.stack([first_row, second_row], 1)


def shards(vectors, conduction, valence, hole_point, kpoint_grid, image_cells):
    group_size = lax.axis_size("kgrp")
    local_k = conduction.shape[0]
    slab_width = conduction.shape[4]
    own_excitons = vectors.shape[1]
    blocks = vectors.shape[2] // group_size
    columns = vectors.reshape(2, own_excitons, group_size, blocks)
    owned_columns = lax.all_to_all(columns, "kgrp", split_axis=2, concat_axis=2, tiled=True)
    owned_columns = owned_columns.reshape(2, own_excitons, local_k, NV, NC)
    hole_offset = hole_point[0] % slab_width
    hole_slab = hole_point[0] // slab_width
    present = (lax.axis_index("img") == hole_slab).astype(jnp.float32)
    picked = (
        lax.dynamic_slice_in_dim(valence[:, :, :, 0, :], hole_offset, 1, 3)[..., 0].astype(
            jnp.float32
        )
        * present
    )
    hole_values = lax.psum(picked, "img")
    all_columns = lax.all_gather(owned_columns, "img", axis=1, tiled=True)
    weights = hole_weights(all_columns, hole_values)
    phases = phase_table(kpoint_grid, image_cells)
    products = jnp.einsum(
        "kasbc,kbcp->sakp",
        mixing(weights),
        conduction[:, :, :, 0, :],
        preferred_element_type=jnp.float32,
    ).astype(jnp.bfloat16)
    summed = jnp.einsum(
        "sakp,akbn->spbn",
        lax.all_to_all(products, "kgrp", split_axis=3, concat_axis=2, tiled=True),
        phases,
        preferred_element_type=jnp.float32,
    )
    normal_scale = (2 * kpoint_grid.shape[1]) ** (-0.5)
    summed = summed * normal_scale
    return (summed[:, None, :, 0, :], summed[:, None, :, 1, :])


def solution(mesh):
    placed = (
        P(None, "img", "kgrp"),
        P("kgrp", None, None, "img", None),
        P("kgrp", None, None, "img", None),
        P(),
        P(),
        P(),
    )
    return jax.shard_map(
        shards,
        mesh=mesh,
        in_specs=placed,
        out_specs=(P(None, "img", "kgrp", None), P(None, "img", "kgrp", None)),
        check_vma=False,
    )
```

profile of v0, /device:TPU:8, one launch (start us, length us, event | category | flops | bytes accessed | tf_op | source)
XLA Modules:
  0.0 111.9 jit_solution(5236022632202495821)
XLA Ops:
  0.6 0.0 copy-start
  0.6 1.5 %copy.29 = f32[2,4,128]{1,0,2:T(2,128)} copy(f32[2,4,128]{2,1,0:T(4,128)} %param.6) | data formatting | bytes 8192 | tf_op args[0]
  2.2 19.8 %all-to-all-start = ((f32[2,4,128,1]{1,0,3,2:T(2,128)}), f32[2,4,128,1]{1,0,3,2:T(2,128)S(1)}, u32[]{:S(2)}, u32[]{:S(2)}) async-start(f32[2,4,128,1]{1,0,3,2:T(2,128)} %bitcast.4), calls=%async_computation | async-start | bytes 262144 | tf_op jit(solution)/shard_map/all_to_all | solution.py:64
  22.7 0.9 multiply_reduce_fusion
  23.5 6.3 %psum.7 = f32[2,2,8]{2,1,0:T(2,128)S(1)} all-reduce(f32[2,2,8]{2,1,0:T(2,128)S(1)} %multiply_reduce_fusion), channel_id=1, replica_groups=mesh['kgrp'=128,'img'=4] {'img'}, use_global_device_ids=true, to_apply=%region_0.1 | all-reduce | flops 32 | bytes 256 | tf_op jit(solution)/shard_map/psum | solution.py:75
  29.9 6.6 %all-to-all-done = f32[2,4,128,1]{1,0,3,2:T(2,128)S(1)} async-done(((f32[2,4,128,1]{1,0,3,2:T(2,128)}), f32[2,4,128,1]{1,0,3,2:T(2,128)S(1)}, u32[]{:S(2)}, u32[]{:S(2)}) %all-to-all-start) | async-done | bytes 4128 | tf_op jit(solution)/shard_map/all_to_all | solution.py:64
  36.5 0.3 copy.30
  36.8 5.8 %all_gather.3 = f32[2,16,2,8,8]{4,3,2,0,1:T(8,128)S(1)} all-gather(f32[2,4,2,8,8]{4,3,2,0,1:T(8,128)S(1)} %copy.30), channel_id=1, replica_groups=mesh['kgrp'=128,'img'=4] {'img'}, dimensions={1}, use_global_device_ids=true | all-gather | bytes 20480 | tf_op jit(solution)/shard_map/all_gather | solution.py:76
  42.6 0.3 fusion.15
  42.8 0.3 fusion.13
  43.1 0.3 fusion.19
  43.4 0.3 fusion.17
  43.6 0.1 copy.41
  43.7 0.1 copy.44
  43.8 0.1 copy.45
  43.8 0.1 copy.46
  43.9 0.0 copy-done
  43.9 0.3 fusion.1
  44.3 7.1 %copy.32 = bf16[16,2,2,4096]{0,1,2,3:T(2,128)(2,1)} copy(bf16[16,2,2,4096]{3,0,1,2:T(8,128)(2,1)S(1)} %fusion.1) | data formatting | bytes 1048576 | tf_op jit(solution)/shard_map/convert_element_type | solution.py:84
  51.4 0.0 copy-start.2
  51.4 0.0 copy-start.1
  51.4 12.9 %reshape.653 = bf16[128,2,1024]{2,1,0:T(2,128)(2,1)} reshape(bf16[4096,2,2,16]{3,2,1,0:T(2,128)(2,1)} %bitcast.114) | data formatting | bytes 1048576
  64.3 9.2 %all-to-all-start.1 = ((bf16[128,2,1024]{2,1,0:T(2,128)(2,1)}), bf16[128,2,1024]{2,1,0:T(2,128)(2,1)S(1)}, u32[]{:S(2)}, u32[]{:S(2)}) async-start(bf16[128,2,1024]{2,1,0:T(2,128)(2,1)} %reshape.653), calls=%async_computation.1 | async-start | bytes 1048576 | tf_op jit(solution)/shard_map/all_to_all | solution.py:87
  73.5 0.0 copy-done.2
  73.6 0.0 copy-done.1
  73.6 1.1 fusion.12
  74.6 0.1 maximum_bitcast_fusion.2
  74.7 22.0 %all-to-all-done.1 = bf16[128,2,1024]{2,1,0:T(2,128)(2,1)S(1)} async-done(((bf16[128,2,1024]{2,1,0:T(2,128)(2,1)}), bf16[128,2,1024]{2,1,0:T(2,128)(2,1)S(1)}, u32[]{:S(2)}, u32[]{:S(2)}) %all-to-all-start.1) | async-done | bytes 524320 | tf_op jit(solution)/shard_map/all_to_all | solution.py:87
  96.8 4.1 %reshape.654 = bf16[4096,2,2,16]{3,2,1,0:T(2,128)(2,1)} reshape(bf16[128,2,1024]{2,1,0:T(2,128)(2,1)S(1)} %all-to-all-done.1) | data formatting | bytes 1048576
  100.9 8.6 %copy.52 = bf16[16,2,2,128,32]{4,0,2,3,1:T(8,128)(2,1)S(1)} copy(bf16[16,2,2,128,32]{0,1,2,4,3:T(2,128)(2,1)} %bitcast.115) | data formatting | bytes 1048576 | tf_op jit(solution)/shard_map/all_to_all | solution.py:87
  109.5 1.0 bitcast_multiply_fusion
  110.4 1.5 %slice_bitcast_fusion = (f32[16,1,32,512]{3,2,1,0:T(8,128)}, f32[16,1,32,512]{3,2,1,0:T(8,128)}) fusion(f32[16,32,2,512]{3,1,2,0:T(8,128)S(1)} %bitcast_multiply_fusion), kind=kLoop, calls=%fused_computation.6 | loop fusion | bytes 4194304
  (6 shorter events, 0.1 us)
Async XLA Ops:
  0.6 43.3 %copy-start = (bf16[2,2,8,1,4096]{4,2,3,1,0:T(8,128)(2,1)S(1)}, bf16[2,2,8,1,4096]{4,2,3,1,0:T(8,128)(2,1)}, u32[]{:S(2)}) copy-start(bf16[2,2,8,1,4096]{4,2,3,1,0:T(8,128)(2,1)} %param.7) | copy-start | bytes 786436
  2.2 34.3 %all-to-all-start = ((f32[2,4,128,1]{1,0,3,2:T(2,128)}), f32[2,4,128,1]{1,0,3,2:T(2,128)S(1)}, u32[]{:S(2)}, u32[]{:S(2)}) async-start(f32[2,4,128,1]{1,0,3,2:T(2,128)} %bitcast.4), calls=%async_computation | async-start | bytes 262144 | tf_op jit(solution)/shard_map/all_to_all | solution.py:64
  51.4 22.1 %copy-start.2 = (s32[3,256]{1,0:T(4,128)S(1)}, s32[3,256]{1,0:T(4,128)}, u32[]{:S(2)}) copy-start(s32[3,256]{1,0:T(4,128)} %param.10) | copy-start | bytes 9220
  51.4 22.1 %copy-start.1 = (s32[3,512]{1,0:T(4,128)S(1)}, s32[3,512]{1,0:T(4,128)}, u32[]{:S(2)}) copy-start(s32[3,512]{1,0:T(4,128)} %param.11) | copy-start | bytes 18436
  64.3 32.4 %all-to-all-start.1 = ((bf16[128,2,1024]{2,1,0:T(2,128)(2,1)}), bf16[128,2,1024]{2,1,0:T(2,128)(2,1)S(1)}, u32[]{:S(2)}, u32[]{:S(2)}) async-start(bf16[128,2,1024]{2,1,0:T(2,128)(2,1)} %reshape.653), calls=%async_computation.1 | async-start | bytes 1048576 | tf_op jit(solution)/shard_map/all_to_all | solution.py:87
where the time goes:
time: 112 us
  local copies, waits for them, and re-layouts  36.4 us (32%)
  starting transfers between devices  29 us (26%)
  waiting for transfers between devices  28.6 us (26%)
  blocking collectives  12.1 us (11%)
  matrix products  2.31 us (2%)
  other arithmetic  2.02 us (2%)
  between operations  1.47 us (1%)
    all_to_all x1, waiting for transfers between devices, shards(): lax.all_to_all(products, 'kgrp', split_axis=3, concat_axis=2, tiled=True)  22 us
    unnamed x10, local copies, waits for them, and re-layouts  20.1 us
    all_to_all x1, starting transfers between devices, shards(): lax.all_to_all(columns, 'kgrp', split_axis=2, concat_axis=2, tiled=True)  19.8 us
    all_to_all x1, starting transfers between devices, shards(): lax.all_to_all(products, 'kgrp', split_axis=3, concat_axis=2, tiled=True)  9.2 us
    all_to_all x1, local copies, waits for them, and re-layouts, shards(): lax.all_to_all(products, 'kgrp', split_axis=3, concat_axis=2, tiled=True)  8.56 us
    convert_element_type x1, local copies, waits for them, and re-layouts, shards(): products = jnp.einsum('kasbc,kbcp->sakp', mixing(weights), conduction[:,...  7.13 us
    all_to_all x1, waiting for transfers between devices, shards(): lax.all_to_all(columns, 'kgrp', split_axis=2, concat_axis=2, tiled=True)  6.61 us
    psum x1, blocking collectives, shards(): hole_values = lax.psum(picked, 'img')  6.33 us
  transfers between devices with their start and end apart: 2, of which 2 were waited for; matrix products, arithmetic and copies ran while one was open for 2% of the time, Pallas kernels for 0%

commit v1 on v0

--- a/solution.py
+++ b/solution.py
@@ -8,6 +8,11 @@
 NC = 8
 cosine_levels = np.cos(2.0 * np.pi * np.arange(12) / 12.0)
 sine_levels = np.sin(2.0 * np.pi * np.arange(12) / 12.0)
+
+
+def node_run(mat):
+    piece_next = lax.all_gather(mat, "img")
+    return jnp.concatenate(piece_next, axis=1)
 
 
 def phase_table(kpoint_grid, image_cells):
@@ -73,7 +78,7 @@
         * present
     )
     hole_values = lax.psum(picked, "img")
-    all_columns = lax.all_gather(owned_columns, "img", axis=1, tiled=True)
+    all_columns = node_run(owned_columns)
     weights = hole_weights(all_columns, hole_values)
     phases = phase_table(kpoint_grid, image_cells)
     products = jnp.einsum(

time: 112 us -> 112 us (level)
  no operation moved by 1% of the time
where the time goes in v1:
time: 112 us
  local copies, waits for them, and re-layouts  36.4 us (32%)
  starting transfers between devices  29 us (26%)
  waiting for transfers between devices  28.6 us (26%)
  blocking collectives  12.1 us (11%)
  matrix products  2.3 us (2%)
  other arithmetic  2.02 us (2%)
  between operations  1.47 us (1%)
    all_to_all x1, waiting for transfers between devices, shards(): lax.all_to_all(products, 'kgrp', split_axis=3, concat_axis=2, tiled=True)  22 us
    unnamed x10, local copies, waits for them, and re-layouts  20.1 us
    all_to_all x1, starting transfers between devices, shards(): lax.all_to_all(columns, 'kgrp', split_axis=2, concat_axis=2, tiled=True)  19.8 us
    all_to_all x1, starting transfers between devices, shards(): lax.all_to_all(products, 'kgrp', split_axis=3, concat_axis=2, tiled=True)  9.19 us
    all_to_all x1, local copies, waits for them, and re-layouts, shards(): lax.all_to_all(products, 'kgrp', split_axis=3, concat_axis=2, tiled=True)  8.56 us
    convert_element_type x1, local copies, waits for them, and re-layouts, shards(): products = jnp.einsum('kasbc,kbcp->sakp', mixing(weights), conduction[:,...  7.13 us
    all_to_all x1, waiting for transfers between devices, shards(): lax.all_to_all(columns, 'kgrp', split_axis=2, concat_axis=2, tiled=True)  6.61 us
    psum x1, blocking collectives, shards(): hole_values = lax.psum(picked, 'img')  6.33 us
  transfers between devices with their start and end apart: 2, of which 2 were waited for; matrix products, arithmetic and copies ran while one was open for 2% of the time, Pallas kernels for 0%

profile of v1, /device:TPU:8, one launch (start us, length us, event | category | flops | bytes accessed | tf_op | source)
XLA Modules:
  0.0 111.9 jit_solution(3656365119575708401)
XLA Ops:
  0.6 0.0 copy-start
  0.6 1.5 %copy.20 = f32[2,4,128]{1,0,2:T(2,128)} copy(f32[2,4,128]{2,1,0:T(4,128)} %param.6) | data formatting | bytes 8192 | tf_op args[0]
  2.2 19.8 %all-to-all-start = ((f32[2,4,128,1]{1,0,3,2:T(2,128)}), f32[2,4,128,1]{1,0,3,2:T(2,128)S(1)}, u32[]{:S(2)}, u32[]{:S(2)}) async-start(f32[2,4,128,1]{1,0,3,2:T(2,128)} %bitcast.4), calls=%async_computation | async-start | bytes 262144 | tf_op jit(solution)/shard_map/all_to_all | solution.py:69
  22.7 0.9 multiply_reduce_fusion
  23.5 6.3 %psum.7 = f32[2,2,8]{2,1,0:T(2,128)S(1)} all-reduce(f32[2,2,8]{2,1,0:T(2,128)S(1)} %multiply_reduce_fusion), channel_id=1, replica_groups=mesh['kgrp'=128,'img'=4] {'img'}, use_global_device_ids=true, to_apply=%region_0.1 | all-reduce | flops 32 | bytes 256 | tf_op jit(solution)/shard_map/psum | solution.py:80
  29.9 6.6 %all-to-all-done = f32[2,4,128,1]{1,0,3,2:T(2,128)S(1)} async-done(((f32[2,4,128,1]{1,0,3,2:T(2,128)}), f32[2,4,128,1]{1,0,3,2:T(2,128)S(1)}, u32[]{:S(2)}, u32[]{:S(2)}) %all-to-all-start) | async-done | bytes 4128 | tf_op jit(solution)/shard_map/all_to_all | solution.py:69
  36.5 0.3 copy.21
  36.8 5.8 %all_gather.3 = f32[4,2,4,2,8,8]{5,4,3,2,1,0:T(8,128)S(1)} all-gather(f32[1,2,4,2,8,8]{5,4,3,2,1,0:T(8,128)S(1)} %copy.21), channel_id=1, replica_groups=mesh['kgrp'=128,'img'=4] {'img'}, dimensions={0}, use_global_device_ids=true | all-gather | bytes 20480 | tf_op jit(solution)/shard_map/all_gather | solution.py:14
  42.6 0.3 fusion.15
  42.8 0.3 fusion.13
  43.1 0.3 fusion.19
  43.3 0.3 fusion.17
  43.6 0.1 copy.32
  43.7 0.1 copy.35
  43.7 0.1 copy.36
  43.8 0.1 copy.37
  43.9 0.0 copy-done
  43.9 0.3 fusion.1
  44.3 7.1 %copy.23 = bf16[16,2,2,4096]{0,1,2,3:T(2,128)(2,1)} copy(bf16[16,2,2,4096]{3,0,1,2:T(8,128)(2,1)S(1)} %fusion.1) | data formatting | bytes 1048576 | tf_op jit(solution)/shard_map/convert_element_type | solution.py:89
  51.4 0.0 copy-start.2
  51.4 0.0 copy-start.1
  51.4 12.9 %reshape.658 = bf16[128,2,1024]{2,1,0:T(2,128)(2,1)} reshape(bf16[4096,2,2,16]{3,2,1,0:T(2,128)(2,1)} %bitcast.113) | data formatting | bytes 1048576
  64.3 9.2 %all-to-all-start.1 = ((bf16[128,2,1024]{2,1,0:T(2,128)(2,1)}), bf16[128,2,1024]{2,1,0:T(2,128)(2,1)S(1)}, u32[]{:S(2)}, u32[]{:S(2)}) async-start(bf16[128,2,1024]{2,1,0:T(2,128)(2,1)} %reshape.658), calls=%async_computation.1 | async-start | bytes 1048576 | tf_op jit(solution)/shard_map/all_to_all | solution.py:92
  73.5 0.0 copy-done.2
  73.5 0.0 copy-done.1
  73.6 1.1 fusion.12
  74.6 0.1 maximum_bitcast_fusion.2
  74.7 22.0 %all-to-all-done.1 = bf16[128,2,1024]{2,1,0:T(2,128)(2,1)S(1)} async-done(((bf16[128,2,1024]{2,1,0:T(2,128)(2,1)}), bf16[128,2,1024]{2,1,0:T(2,128)(2,1)S(1)}, u32[]{:S(2)}, u32[]{:S(2)}) %all-to-all-start.1) | async-done | bytes 524320 | tf_op jit(solution)/shard_map/all_to_all | solution.py:92
  96.8 4.1 %reshape.659 = bf16[4096,2,2,16]{3,2,1,0:T(2,128)(2,1)} reshape(bf16[128,2,1024]{2,1,0:T(2,128)(2,1)S(1)} %all-to-all-done.1) | data formatting | bytes 1048576
  100.9 8.6 %copy.43 = bf16[16,2,2,128,32]{4,0,2,3,1:T(8,128)(2,1)S(1)} copy(bf16[16,2,2,128,32]{0,1,2,4,3:T(2,128)(2,1)} %bitcast.114) | data formatting | bytes 1048576 | tf_op jit(solution)/shard_map/all_to_all | solution.py:92
  109.4 0.9 bitcast_multiply_fusion
  110.4 1.5 %slice_bitcast_fusion = (f32[16,1,32,512]{3,2,1,0:T(8,128)}, f32[16,1,32,512]{3,2,1,0:T(8,128)}) fusion(f32[16,32,2,512]{3,1,2,0:T(8,128)S(1)} %bitcast_multiply_fusion), kind=kLoop, calls=%fused_computation.6 | loop fusion | bytes 4194304
  (6 shorter events, 0.1 us)
Async XLA Ops:
  0.6 43.3 %copy-start = (bf16[2,2,8,1,4096]{4,2,3,1,0:T(8,128)(2,1)S(1)}, bf16[2,2,8,1,4096]{4,2,3,1,0:T(8,128)(2,1)}, u32[]{:S(2)}) copy-start(bf16[2,2,8,1,4096]{4,2,3,1,0:T(8,128)(2,1)} %param.7) | copy-start | bytes 786436
  2.2 34.3 %all-to-all-start = ((f32[2,4,128,1]{1,0,3,2:T(2,128)}), f32[2,4,128,1]{1,0,3,2:T(2,128)S(1)}, u32[]{:S(2)}, u32[]{:S(2)}) async-start(f32[2,4,128,1]{1,0,3,2:T(2,128)} %bitcast.4), calls=%async_computation | async-start | bytes 262144 | tf_op jit(solution)/shard_map/all_to_all | solution.py:69
  51.4 22.1 %copy-start.2 = (s32[3,256]{1,0:T(4,128)S(1)}, s32[3,256]{1,0:T(4,128)}, u32[]{:S(2)}) copy-start(s32[3,256]{1,0:T(4,128)} %param.10) | copy-start | bytes 9220
  51.4 22.1 %copy-start.1 = (s32[3,512]{1,0:T(4,128)S(1)}, s32[3,512]{1,0:T(4,128)}, u32[]{:S(2)}) copy-start(s32[3,512]{1,0:T(4,128)} %param.11) | copy-start | bytes 18436
  64.3 32.4 %all-to-all-start.1 = ((bf16[128,2,1024]{2,1,0:T(2,128)(2,1)}), bf16[128,2,1024]{2,1,0:T(2,128)(2,1)S(1)}, u32[]{:S(2)}, u32[]{:S(2)}) async-start(bf16[128,2,1024]{2,1,0:T(2,128)(2,1)} %reshape.658), calls=%async_computation.1 | async-start | bytes 1048576 | tf_op jit(solution)/shard_map/all_to_all | solution.py:92
